TPU v7x, 32 devices: a whole 2x2x4 slice. The times are simulated.
32 devices in a mesh: pb: 2 (over x), ka: 16 (over z, y, core).
Axes of the slice: x: 2, y: 2, z: 4, core: 2. Of those that a mesh axis runs over, the one named last changes fastest.
Arguments:
- coupling: bfloat16 [2, 16, 32, 32, 384], P('pb', 'ka'), may hold values from -0.796875 to 0.796875
- phonon_occ: float32 [2, 16, 32, 12], P('pb', 'ka'), may hold values from 0.1 to 1
- band_window: int32 [2, 16, 32, 32], P('pb', 'ka'), may hold values 0 or 1
- pair_count: int32 [2, 16, 16], P('pb', 'ka'), may hold values from 0 to 2, as said below
- k_target: int32 [2, 16, 32], P('pb', 'ka'), may hold values from 0 to 127
- kq_source: int32 [2, 16, 32], P('pb', 'ka'), may hold values from 0 to 127
- velocity: float32 [3, 32, 2048], P(None, None, 'ka'), may hold values from -6 to 6
- lifetime: float32 [32, 2048], P(None, 'ka'), may hold values from 0.5 to 2
Outputs:
- deviation: float32 [3, 32, 2048], P(None, None, 'ka')
Inputs may be any that keep to these rules, and one draw needn't show every extreme that they name: pair_count[p, a, d] is the number of live tile slots among slots d * 2 to d * 2 + 1 of device (p, a); in every q-group p some owner d receives 2 live tiles from every source.
All inputs are finite; a program needn't handle non-finite values. No bound on the sum of `band_window` on one device may be relied on, other than what follows from the above.
Results may differ from a plain program's by a relative error of at most 0.012.
Values may be sent and summed in bfloat16 or wider, within the bound.
A program may use at most 64 MiB of HBM per device.

v0:
```python
import jax
import jax.numpy as jnp
from jax import lax
from jax.sharding import PartitionSpec as P

MODES = 12
TILE_SLOTS = 2
ITERS = 4


def tile_terms(weight, chosen):
    return jnp.einsum("tnm,dmt->dnt", weight, chosen, preferred_element_type=jnp.float32)


def shards(coupling, phonon_occ, band_window, pair_count, k_target, kq_source, velocity, lifetime):
    tile_count = coupling.shape[2]
    block_width = velocity.shape[2]
    directions = velocity.shape[0]
    band_count = velocity.shape[1]
    slot_live = (
        (jnp.arange(TILE_SLOTS)[None, :] < pair_count[0, 0][:, None])
        .reshape(tile_count)
        .astype(jnp.float32)
    )
    window = band_window[0, 0].astype(jnp.float32) * slot_live[:, None]
    widened = coupling[0, 0].astype(jnp.float32)
    squared = (widened * widened).reshape(tile_count, band_count, band_count, MODES)
    summed = jnp.sum(squared * phonon_occ[0, 0][:, None, None, :], axis=3)
    weight = (summed * window[:, :, None]).astype(jnp.bfloat16)
    targets = lax.all_to_all(k_target[0, 0], "ka", split_axis=0, concat_axis=0, tiled=True)
    onehot = (targets[:, None] == jnp.arange(block_width, dtype=jnp.int32)[None, :]).astype(
        jnp.float32
    )
    deviation = lifetime[None] * velocity
    for iteration in range(ITERS):
        rounded = deviation.astype(jnp.bfloat16)
        local_terms = tile_terms(weight, jnp.take(rounded, kq_source[0, 0], axis=2))
        contribution = lax.all_to_all(
            local_terms.astype(jnp.bfloat16), "ka", split_axis=2, concat_axis=2, tiled=True
        ).astype(local_terms.dtype)
        partial_value = jnp.dot(
            contribution.reshape(directions * band_count, tile_count),
            onehot,
            precision=lax.Precision.HIGHEST,
            preferred_element_type=jnp.float32,
        )
        partial_value = partial_value.reshape(directions, band_count, block_width)
        scattering = lax.psum(partial_value.astype(jnp.bfloat16), "pb").astype(jnp.float32)
        deviation = lifetime[None] * (velocity + scattering)
    return deviation


def solution(mesh):
    placed = (
        P("pb", "ka", None, None, None),
        P("pb", "ka", None, None),
        P("pb", "ka", None, None),
        P("pb", "ka", None),
        P("pb", "ka", None),
        P("pb", "ka", None),
        P(None, None, "ka"),
        P(None, "ka"),
    )
    return jax.shard_map(
        shards, mesh=mesh, in_specs=placed, out_specs=P(None, None, "ka"), check_vma=False
    )
```

profile of v0, /device:TPU:0, one launch (start us, length us, event | category | flops | bytes accessed | tf_op | source)
XLA Modules:
  0.0 100.8 jit_solution(7904888660373477923)
XLA Ops:
  0.5 1.3 %reduce.6 = s32[32]{0:T(128)S(1)} reduce(s32[1,1,32]{2,1,0:T(1,128)} %param.14, s32[]{:T(128)} %broadcast.93), dimensions={0,1}, to_apply=%param.14.reduce_sub_computation.3 | reduce | bytes 260 | tf_op args[4]
  1.9 0.7 all_to_all.19
  2.5 7.4 %all-to-all-start.1 = ((s32[16,2,1]{1,2,0:T(1,128)}), s32[16,2,1]{1,2,0:T(1,128)S(1)}, u32[]{:S(2)}, u32[]{:S(2)}) async-start(s32[16,2,1]{1,2,0:T(1,128)} %bitcast.6), calls=%async_computation.1 | async-start | bytes 16384 | tf_op jit(solution)/shard_map/all_to_all | solution.py:30
  10.0 0.7 compare_select_fusion
  10.6 0.7 compare_and_fusion
  11.3 1.3 %convert_multiply_fusion = f32[1,1,32,32,384]{4,3,2,1,0:T(8,128)S(1)} fusion(bf16[1,1,32,32,384]{4,3,2,1,0:T(8,128)(2,1)} %param.10), kind=kLoop, calls=%fused_computation.5 | loop fusion | flops 786432 | bytes 2359296 | tf_op jit(solution)/shard_map/mul | solution.py:27
  12.6 5.9 %copy.30 = f32[1,1,32,32,384]{3,2,4,1,0:T(8,128)} copy(f32[1,1,32,32,384]{4,3,2,1,0:T(8,128)S(1)} %convert_multiply_fusion) | data formatting | bytes 3145728 | tf_op jit(solution)/shard_map/mul | solution.py:27
  18.8 3.7 %multiply_reduce_fusion = f32[32,32,32]{1,0,2:T(8,128)S(1)} fusion(f32[32,32,32,12]{1,0,3,2:T(8,128)} %bitcast.43, f32[32,12]{0,1:T(8,128)S(1)} %bitcast.44), kind=kLoop, calls=%fused_computation.4 | loop fusion | flops 753664 | bytes 1705472 | tf_op jit(solution)/shard_map/reduce_sum | solution.py:28
  23.1 0.6 gather_fusion
  23.7 0.9 fusion
  24.7 6.0 %all-to-all-start = ((bf16[3,32,32]{1,0,2:T(4,128)(2,1)}), bf16[3,32,32]{1,0,2:T(4,128)(2,1)S(1)}, u32[]{:S(2)}, u32[]{:S(2)}) async-start(bf16[3,32,32]{1,0,2:T(4,128)(2,1)} %fusion), calls=%async_computation | async-start | bytes 65536 | tf_op jit(solution)/shard_map/all_to_all | solution.py:38
  30.7 0.7 reduce.7
  31.5 5.9 %all-to-all-done = bf16[3,32,32]{1,0,2:T(4,128)(2,1)S(1)} async-done(((bf16[3,32,32]{1,0,2:T(4,128)(2,1)}), bf16[3,32,32]{1,0,2:T(4,128)(2,1)S(1)}, u32[]{:S(2)}, u32[]{:S(2)}) %all-to-all-start) | async-done | bytes 6176 | tf_op jit(solution)/shard_map/all_to_all | solution.py:38
  37.5 8.4 %psum.28 = bf16[3,32,128]{2,1,0:T(8,128)(2,1)S(1)} all-reduce(bf16[3,32,128]{2,1,0:T(8,128)(2,1)S(1)} %convolution_convert_fusion.7), channel_id=1, replica_groups=mesh['pb'=2,'ka'=16] {'pb'}, use_global_device_ids=true, to_apply=%region_1.0 | all-reduce | flops 12288 | bytes 49152 | tf_op jit(solution)/shard_map/psum | solution.py:48
  46.0 0.6 gather_fusion.1
  47.0 9.2 %all_to_all.29 = bf16[3,32,32]{1,0,2:T(4,128)(2,1)S(1)} all-to-all(bf16[3,32,32]{1,0,2:T(4,128)(2,1)S(1)} %fusion.1), channel_id=1, replica_groups=mesh['pb'=2,'ka'=16] {'ka'}, dimensions={2} | all-to-all | bytes 12288 | tf_op jit(solution)/shard_map/all_to_all | solution.py:38
  56.3 7.3 %psum.29 = bf16[3,32,128]{2,1,0:T(8,128)(2,1)S(1)} all-reduce(bf16[3,32,128]{2,1,0:T(8,128)(2,1)S(1)} %convolution_convert_fusion.6), channel_id=1, replica_groups=mesh['pb'=2,'ka'=16] {'pb'}, use_global_device_ids=true, to_apply=%region_2.4 | all-reduce | flops 12288 | bytes 49152 | tf_op jit(solution)/shard_map/psum | solution.py:48
  63.8 0.6 gather_fusion.2
  64.7 9.2 %all_to_all.30 = bf16[3,32,32]{1,0,2:T(4,128)(2,1)S(1)} all-to-all(bf16[3,32,32]{1,0,2:T(4,128)(2,1)S(1)} %fusion.2), channel_id=1, replica_groups=mesh['pb'=2,'ka'=16] {'ka'}, dimensions={2} | all-to-all | bytes 12288 | tf_op jit(solution)/shard_map/all_to_all | solution.py:38
  74.1 8.5 %psum.30 = bf16[3,32,128]{2,1,0:T(8,128)(2,1)S(1)} all-reduce(bf16[3,32,128]{2,1,0:T(8,128)(2,1)S(1)} %convolution_convert_fusion.5), channel_id=1, replica_groups=mesh['pb'=2,'ka'=16] {'pb'}, use_global_device_ids=true, to_apply=%region_3.5 | all-reduce | flops 12288 | bytes 49152 | tf_op jit(solution)/shard_map/psum | solution.py:48
  82.7 0.6 gather_fusion.3
  83.6 9.2 %all_to_all.31 = bf16[3,32,32]{1,0,2:T(4,128)(2,1)S(1)} all-to-all(bf16[3,32,32]{1,0,2:T(4,128)(2,1)S(1)} %fusion.3), channel_id=1, replica_groups=mesh['pb'=2,'ka'=16] {'ka'}, dimensions={2} | all-to-all | bytes 12288 | tf_op jit(solution)/shard_map/all_to_all | solution.py:38
  93.0 7.1 %psum.31 = bf16[3,32,128]{2,1,0:T(8,128)(2,1)S(1)} all-reduce(bf16[3,32,128]{2,1,0:T(8,128)(2,1)S(1)} %convolution_convert_fusion.4), channel_id=1, replica_groups=mesh['pb'=2,'ka'=16] {'pb'}, use_global_device_ids=true, to_apply=%region_4.6 | all-reduce | flops 12288 | bytes 49152 | tf_op jit(solution)/shard_map/psum | solution.py:48
  100.1 0.6 add_multiply_fusion
  (35 shorter events, 3.6 us)
Async XLA Ops:
  0.0 18.6 %copy-start.3 = (f32[1,1,32,12]{2,1,3,0:T(1,128)S(1)}, f32[1,1,32,12]{2,1,3,0:T(1,128)}, u32[]{:S(2)}) copy-start(f32[1,1,32,12]{2,1,3,0:T(1,128)} %param.11) | copy-start | bytes 4612
  0.0 18.6 %copy-start.4 = (s32[1,1,16]{2,1,0:T(1,128)S(1)}, s32[1,1,16]{2,1,0:T(1,128)}, u32[]{:S(2)}) copy-start(s32[1,1,16]{2,1,0:T(1,128)} %param.13) | copy-start | bytes 196
  2.5 22.1 %all-to-all-start.1 = ((s32[16,2,1]{1,2,0:T(1,128)}), s32[16,2,1]{1,2,0:T(1,128)S(1)}, u32[]{:S(2)}, u32[]{:S(2)}) async-start(s32[16,2,1]{1,2,0:T(1,128)} %bitcast.6), calls=%async_computation.1 | async-start | bytes 16384 | tf_op jit(solution)/shard_map/all_to_all | solution.py:30
  12.6 9.9 %copy-start.2 = (s32[1,1,32,32]{3,2,1,0:T(8,128)S(1)}, s32[1,1,32,32]{3,2,1,0:T(8,128)}, u32[]{:S(2)}) copy-start(s32[1,1,32,32]{3,2,1,0:T(8,128)} %param.12) | copy-start | bytes 12292
  12.6 10.3 %copy-start = (f32[3,32,128]{2,1,0:T(8,128)S(1)}, f32[3,32,128]{2,1,0:T(8,128)}, u32[]{:S(2)}) copy-start(f32[3,32,128]{2,1,0:T(8,128)} %param.16) | copy-start | bytes 147460
  12.6 10.3 %copy-start.1 = (f32[32,128]{1,0:T(8,128)S(1)}, f32[32,128]{1,0:T(8,128)}, u32[]{:S(2)}) copy-start(f32[32,128]{1,0:T(8,128)} %param.17) | copy-start | bytes 49156
  24.7 12.6 %all-to-all-start = ((bf16[3,32,32]{1,0,2:T(4,128)(2,1)}), bf16[3,32,32]{1,0,2:T(4,128)(2,1)S(1)}, u32[]{:S(2)}, u32[]{:S(2)}) async-start(bf16[3,32,32]{1,0,2:T(4,128)(2,1)} %fusion), calls=%async_computation | async-start | bytes 65536 | tf_op jit(solution)/shard_map/all_to_all | solution.py:38
where the time goes:
time: 101 us
  blocking collectives  58.8 us (58%)
  starting transfers between devices  13.4 us (13%)
  local copies, waits for them, and re-layouts  10.7 us (11%)
  other arithmetic  9.2 us (9%)
  waiting for transfers between devices  5.88 us (6%)
  matrix products  2.6 us (3%)
    psum x4, blocking collectives, shards(): lax.psum(partial_value.astype(jnp.bfloat16), 'pb').astype(jnp.float32)  31.2 us
    all_to_all x3, blocking collectives, shards(): lax.all_to_all(local_terms.astype(jnp.bfloat16), 'ka', split_axis=2, conc...  27.6 us
    all_to_all x1, starting transfers between devices, shards(): lax.all_to_all(k_target[0, 0], 'ka', split_axis=0, concat_axis=0, tiled=T...  7.41 us
    all_to_all x1, starting transfers between devices, shards(): lax.all_to_all(local_terms.astype(jnp.bfloat16), 'ka', split_axis=2, conc...  6.01 us
    mul x1, local copies, waits for them, and re-layouts, shards(): widened * widened  5.94 us
    all_to_all x1, waiting for transfers between devices, shards(): lax.all_to_all(local_terms.astype(jnp.bfloat16), 'ka', split_axis=2, conc...  5.88 us
    reduce_sum x1, other arithmetic, shards(): summed = jnp.sum(squared * phonon_occ[0, 0][:, None, None, :], axis=3)  3.71 us
    gather x4, local copies, waits for them, and re-layouts, shards(): local_terms = tile_terms(weight, jnp.take(rounded, kq_source[0, 0], axis=2))  2.44 us
  transfers between devices with their start and end apart: 2, of which 1 were waited for; matrix products, arithmetic and copies ran while one was open for 15% of the time, Pallas kernels for 0%

commit v1 on v0

--- a/solution.py
+++ b/solution.py
@@ -35,9 +35,16 @@
     for iteration in range(ITERS):
         rounded = deviation.astype(jnp.bfloat16)
         local_terms = tile_terms(weight, jnp.take(rounded, kq_source[0, 0], axis=2))
-        contribution = lax.all_to_all(
-            local_terms.astype(jnp.bfloat16), "ka", split_axis=2, concat_axis=2, tiled=True
-        ).astype(local_terms.dtype)
+
+        def draw_edge_for(shard_in):
+            return jnp.concatenate(
+                lax.all_to_all(
+                    jnp.stack(jnp.split(shard_in, lax.axis_size("ka"), axis=2)), "ka", 0, 0
+                ),
+                axis=2,
+            )
+
+        contribution = draw_edge_for(local_terms.astype(jnp.bfloat16)).astype(local_terms.dtype)
         partial_value = jnp.dot(
             contribution.reshape(directions * band_count, tile_count),
             onehot,

time: 101 us -> 102 us (level)
  local copies, waits for them, and re-layouts: 10.7 us -> 12.2 us
where the time goes in v1:
time: 102 us
  blocking collectives  58.6 us (57%)
  starting transfers between devices  13.4 us (13%)
  local copies, waits for them, and re-layouts  12.2 us (12%)
  other arithmetic  9.2 us (9%)
  waiting for transfers between devices  5.82 us (6%)
  matrix products  1.99 us (2%)
    psum x4, blocking collectives, shards(): lax.psum(partial_value.astype(jnp.bfloat16), 'pb').astype(jnp.float32)  31.2 us
    all_to_all x3, blocking collectives, draw_edge_for(): lax.all_to_all(jnp.stack(jnp.split(shard_in, lax.axis_size('ka'), axis=2)...  27.4 us
    all_to_all x1, starting transfers between devices, shards(): lax.all_to_all(k_target[0, 0], 'ka', split_axis=0, concat_axis=0, tiled=T...  7.41 us
    all_to_all x1, starting transfers between devices, draw_edge_for(): lax.all_to_all(jnp.stack(jnp.split(shard_in, lax.axis_size('ka'), axis=2)...  6.01 us
    mul x1, local copies, waits for them, and re-layouts, shards(): widened * widened  5.94 us
    all_to_all x1, waiting for transfers between devices, draw_edge_for(): lax.all_to_all(jnp.stack(jnp.split(shard_in, lax.axis_size('ka'), axis=2)...  5.81 us
    reduce_sum x1, other arithmetic, shards(): summed = jnp.sum(squared * phonon_occ[0, 0][:, None, None, :], axis=3)  3.71 us
    gather x4, local copies, waits for them, and re-layouts, shards(): local_terms = tile_terms(weight, jnp.take(rounded, kq_source[0, 0], axis=2))  2.44 us
  transfers between devices with their start and end apart: 2, of which 1 were waited for; matrix products, arithmetic and copies ran while one was open for 15% of the time, Pallas kernels for 0%

profile of v1, /device:TPU:0, one launch (start us, length us, event | category | flops | bytes accessed | tf_op | source)
XLA Modules:
  0.0 101.5 jit_solution(10398023093548167024)
XLA Ops:
  0.5 1.3 %reduce.6 = s32[32]{0:T(128)S(1)} reduce(s32[1,1,32]{2,1,0:T(1,128)} %param.14, s32[]{:T(128)} %broadcast.93), dimensions={0,1}, to_apply=%param.14.reduce_sub_computation.3 | reduce | bytes 260 | tf_op args[4]
  1.9 0.7 all_to_all.19
  2.5 7.4 %all-to-all-start.1 = ((s32[16,2,1]{1,2,0:T(1,128)}), s32[16,2,1]{1,2,0:T(1,128)S(1)}, u32[]{:S(2)}, u32[]{:S(2)}) async-start(s32[16,2,1]{1,2,0:T(1,128)} %bitcast.24), calls=%async_computation.1 | async-start | bytes 16384 | tf_op jit(solution)/shard_map/all_to_all | solution.py:30
  10.0 0.7 compare_select_fusion
  10.6 0.7 compare_and_fusion
  11.3 1.3 %convert_multiply_fusion = f32[1,1,32,32,384]{4,3,2,1,0:T(8,128)S(1)} fusion(bf16[1,1,32,32,384]{4,3,2,1,0:T(8,128)(2,1)} %param.10), kind=kLoop, calls=%fused_computation.5 | loop fusion | flops 786432 | bytes 2359296 | tf_op jit(solution)/shard_map/mul | solution.py:27
  12.6 5.9 %copy.62 = f32[1,1,32,32,384]{3,2,4,1,0:T(8,128)} copy(f32[1,1,32,32,384]{4,3,2,1,0:T(8,128)S(1)} %convert_multiply_fusion) | data formatting | bytes 3145728 | tf_op jit(solution)/shard_map/mul | solution.py:27
  18.8 3.7 %multiply_reduce_fusion = f32[32,32,32]{1,0,2:T(8,128)S(1)} fusion(f32[32,32,32,12]{1,0,3,2:T(8,128)} %bitcast.311, f32[32,12]{0,1:T(8,128)S(1)} %bitcast.316), kind=kLoop, calls=%fused_computation.4 | loop fusion | flops 753664 | bytes 1705472 | tf_op jit(solution)/shard_map/reduce_sum | solution.py:28
  23.1 0.6 gather_fusion
  24.3 0.6 copy.64
  24.9 6.0 %all-to-all-start = ((bf16[16,3,32,2]{2,3,1,0:T(2,128)(2,1)}), bf16[16,3,32,2]{2,3,1,0:T(2,128)(2,1)S(1)}, u32[]{:S(2)}, u32[]{:S(2)}) async-start(bf16[16,3,32,2]{2,3,1,0:T(2,128)(2,1)} %copy.64), calls=%async_computation | async-start | bytes 49152 | tf_op jit(solution)/shard_map/all_to_all | solution.py:41
  30.9 0.7 reduce.7
  31.7 5.8 %all-to-all-done = bf16[16,3,32,2]{2,3,1,0:T(2,128)(2,1)S(1)} async-done(((bf16[16,3,32,2]{2,3,1,0:T(2,128)(2,1)}), bf16[16,3,32,2]{2,3,1,0:T(2,128)(2,1)S(1)}, u32[]{:S(2)}, u32[]{:S(2)}) %all-to-all-start) | async-done | bytes 6176 | tf_op jit(solution)/shard_map/all_to_all | solution.py:41
  37.7 8.3 %psum.28 = bf16[3,32,128]{2,1,0:T(8,128)(2,1)S(1)} all-reduce(bf16[3,32,128]{2,1,0:T(8,128)(2,1)S(1)} %convolution_convert_fusion.7), channel_id=1, replica_groups=mesh['pb'=2,'ka'=16] {'pb'}, use_global_device_ids=true, to_apply=%region_1.0 | all-reduce | flops 12288 | bytes 49152 | tf_op jit(solution)/shard_map/psum | solution.py:55
  46.2 0.6 gather_fusion.1
  47.3 9.1 %all_to_all.29 = bf16[16,3,32,2]{2,3,1,0:T(2,128)(2,1)S(1)} all-to-all(bf16[16,3,32,2]{2,3,1,0:T(2,128)(2,1)S(1)} %copy.70), channel_id=1, replica_groups=mesh['pb'=2,'ka'=16] {'ka'}, dimensions={0} | all-to-all | bytes 12288 | tf_op jit(solution)/shard_map/all_to_all | solution.py:41
  56.7 7.3 %psum.29 = bf16[3,32,128]{2,1,0:T(8,128)(2,1)S(1)} all-reduce(bf16[3,32,128]{2,1,0:T(8,128)(2,1)S(1)} %convolution_convert_fusion.6), channel_id=1, replica_groups=mesh['pb'=2,'ka'=16] {'pb'}, use_global_device_ids=true, to_apply=%region_2.4 | all-reduce | flops 12288 | bytes 49152 | tf_op jit(solution)/shard_map/psum | solution.py:55
  64.1 0.6 gather_fusion.2
  65.3 9.1 %all_to_all.30 = bf16[16,3,32,2]{2,3,1,0:T(2,128)(2,1)S(1)} all-to-all(bf16[16,3,32,2]{2,3,1,0:T(2,128)(2,1)S(1)} %copy.75), channel_id=1, replica_groups=mesh['pb'=2,'ka'=16] {'ka'}, dimensions={0} | all-to-all | bytes 12288 | tf_op jit(solution)/shard_map/all_to_all | solution.py:41
  74.6 8.5 %psum.30 = bf16[3,32,128]{2,1,0:T(8,128)(2,1)S(1)} all-reduce(bf16[3,32,128]{2,1,0:T(8,128)(2,1)S(1)} %convolution_convert_fusion.5), channel_id=1, replica_groups=mesh['pb'=2,'ka'=16] {'pb'}, use_global_device_ids=true, to_apply=%region_3.5 | all-reduce | flops 12288 | bytes 49152 | tf_op jit(solution)/shard_map/psum | solution.py:55
  83.3 0.6 gather_fusion.3
  84.4 9.1 %all_to_all.31 = bf16[16,3,32,2]{2,3,1,0:T(2,128)(2,1)S(1)} all-to-all(bf16[16,3,32,2]{2,3,1,0:T(2,128)(2,1)S(1)} %copy.80), channel_id=1, replica_groups=mesh['pb'=2,'ka'=16] {'ka'}, dimensions={0} | all-to-all | bytes 12288 | tf_op jit(solution)/shard_map/all_to_all | solution.py:41
  93.8 7.1 %psum.31 = bf16[3,32,128]{2,1,0:T(8,128)(2,1)S(1)} all-reduce(bf16[3,32,128]{2,1,0:T(8,128)(2,1)S(1)} %convolution_convert_fusion.4), channel_id=1, replica_groups=mesh['pb'=2,'ka'=16] {'pb'}, use_global_device_ids=true, to_apply=%region_4.6 | all-reduce | flops 12288 | bytes 49152 | tf_op jit(solution)/shard_map/psum | solution.py:55
  100.9 0.6 add_multiply_fusion
  (107 shorter events, 4.7 us)
Async XLA Ops:
  0.0 18.6 %copy-start.3 = (f32[1,1,32,12]{2,1,3,0:T(1,128)S(1)}, f32[1,1,32,12]{2,1,3,0:T(1,128)}, u32[]{:S(2)}) copy-start(f32[1,1,32,12]{2,1,3,0:T(1,128)} %param.11) | copy-start | bytes 4612
  0.0 18.6 %copy-start.4 = (s32[1,1,16]{2,1,0:T(1,128)S(1)}, s32[1,1,16]{2,1,0:T(1,128)}, u32[]{:S(2)}) copy-start(s32[1,1,16]{2,1,0:T(1,128)} %param.13) | copy-start | bytes 196
  2.5 22.4 %all-to-all-start.1 = ((s32[16,2,1]{1,2,0:T(1,128)}), s32[16,2,1]{1,2,0:T(1,128)S(1)}, u32[]{:S(2)}, u32[]{:S(2)}) async-start(s32[16,2,1]{1,2,0:T(1,128)} %bitcast.24), calls=%async_computation.1 | async-start | bytes 16384 | tf_op jit(solution)/shard_map/all_to_all | solution.py:30
  12.6 9.9 %copy-start.2 = (s32[1,1,32,32]{3,2,1,0:T(8,128)S(1)}, s32[1,1,32,32]{3,2,1,0:T(8,128)}, u32[]{:S(2)}) copy-start(s32[1,1,32,32]{3,2,1,0:T(8,128)} %param.12) | copy-start | bytes 12292
  12.6 10.3 %copy-start = (f32[3,32,128]{2,1,0:T(8,128)S(1)}, f32[3,32,128]{2,1,0:T(8,128)}, u32[]{:S(2)}) copy-start(f32[3,32,128]{2,1,0:T(8,128)} %param.16) | copy-start | bytes 147460
  12.6 10.3 %copy-start.1 = (f32[32,128]{1,0:T(8,128)S(1)}, f32[32,128]{1,0:T(8,128)}, u32[]{:S(2)}) copy-start(f32[32,128]{1,0:T(8,128)} %param.17) | copy-start | bytes 49156
  24.9 12.6 %all-to-all-start = ((bf16[16,3,32,2]{2,3,1,0:T(2,128)(2,1)}), bf16[16,3,32,2]{2,3,1,0:T(2,128)(2,1)S(1)}, u32[]{:S(2)}, u32[]{:S(2)}) async-start(bf16[16,3,32,2]{2,3,1,0:T(2,128)(2,1)} %copy.64), calls=%async_computation | async-start | bytes 49152 | tf_op jit(solution)/shard_map/all_to_all | solution.py:41
